TPU v7x, 32 devices: a whole 2x2x4 slice. The times are simulated.
32 devices in a mesh: aa: 8 (over y, x, core), ba: 4 (over z).
Axes of the slice: x: 2, y: 2, z: 4, core: 2. Of those that a mesh axis runs over, the one named last changes fastest.
Arguments:
- queries: bfloat16 [4, 128, 8192], P('ba', None, 'aa'), may hold values from -10 to 10
- new_kv: bfloat16 [4, 128, 2, 512], P('ba', 'aa'), may hold values from -4 to 4
- pool: bfloat16 [4, 64, 32, 2, 512], P('ba', 'aa'), may hold values from -4 to 4
- page_table: int32 [4, 32], P('ba', 'aa'), may hold values from 0 to 7, as said below
- ctx_len: int32 [4, 8], P('ba', 'aa'), may hold values from 1 to 128, as said below
- move_page: int32 [4, 24], P('ba', 'aa'), may hold values from 0 to 7, as said below
- move_dest: int32 [4, 24], P('ba', 'aa'), may hold values from 0 to 3, as said below
- append_page: int32 [4, 8], P('ba', 'aa'), may hold values from 0 to 7
Outputs:
- attended: bfloat16 [4, 128, 8192], P('ba', None, 'aa')
- pool_out: bfloat16 [4, 64, 32, 2, 512], P('ba', 'aa')
Inputs may be any that keep to these rules, and one draw needn't show every extreme that they name: `page_table`: the entries of one device are distinct pages of its pool and differ from its leaving pages and its append page. `ctx_len`: for each instance some index of aa holds exactly 128 live rows. `move_page`: the 3 entries of one device are distinct pages of its pool. `move_dest`: A device never names its own instance and names any one instance at most 2 times; for each index of aa one instance is named exactly 2 times by the device of every other instance.
All inputs are finite; a program needn't handle non-finite values.
Results may differ from a plain program's by a relative error of at most 0.0017.
Values may be sent and summed in bfloat16 or wider, within the bound.
A program may use at most 64 MiB of HBM per device.

v0:
```python
import math

import jax
import jax.numpy as jnp
from jax import lax
from jax.sharding import PartitionSpec as P

HEAD_DIM = 128
MOST = 2


NEG_LARGE = -1e30


def block_plan(total_rows):
    counted = max(1, total_rows // 512)
    length = -(-total_rows // counted)
    length = -(-length // 8) * 8
    return (counted, length)


def attend_rows(query_heads, key_rows, visible):
    total_rows = key_rows.shape[0]
    counted, length = block_plan(total_rows)
    query_count, kv_heads, group_size, head_dim = query_heads.shape
    blocked_keys = key_rows.reshape(counted, length, 2, kv_heads, head_dim)
    blocked_mask = visible.reshape(query_count, counted, length).transpose(1, 0, 2)
    scale = 1.0 / math.sqrt(head_dim)

    def block_step(state_now, inputs):
        run_max, run_sum, run_out = state_now
        block_keys, block_mask = inputs
        scores = (
            jnp.einsum(
                "qkgd,rkd->qkgr", query_heads, block_keys[:, 0], preferred_element_type=jnp.float32
            )
            * scale
        )
        allowed = block_mask[:, None, None, :]
        scores = jnp.where(allowed, scores, NEG_LARGE)
        new_max = jnp.maximum(run_max, jnp.max(scores, axis=-1))
        weights = jnp.where(allowed, jnp.exp(scores - new_max[..., None]), 0.0)
        shrink = jnp.exp(run_max - new_max)
        new_sum = run_sum * shrink + jnp.sum(weights, axis=-1)
        block_values = block_keys[:, 1].astype(jnp.float32)
        new_out = run_out * shrink[..., None] + jnp.einsum(
            "qkgr,rkd->qkgd", weights, block_values, precision=lax.Precision.HIGHEST
        )
        return ((new_max, new_sum, new_out), None)

    start_state = (
        jnp.full((query_count, kv_heads, group_size), NEG_LARGE, jnp.float32),
        jnp.zeros((query_count, kv_heads, group_size), jnp.float32),
        jnp.zeros((query_count, kv_heads, group_size, head_dim), jnp.float32),
    )
    finished, _ = lax.scan(block_step, start_state, (blocked_keys, blocked_mask))
    return finished


def local(queries, new_kv, pool, page_table, ctx_len, move_page, move_dest, append_page):
    instances = lax.axis_size("ba")
    position = lax.axis_index("aa")
    pool_pages = pool[0]
    page_rows = pool_pages.shape[1]
    kv_width = pool_pages.shape[-1]
    kv_heads = kv_width // HEAD_DIM
    gathered = lax.all_gather(queries[0], "aa", axis=1, tiled=True)
    query_count = gathered.shape[0]
    query_heads = gathered.reshape(query_count, kv_heads, -1, HEAD_DIM)
    moved_ids = move_page[0]
    targets = move_dest[0]
    move_count = moved_ids.shape[0]
    counter = jnp.arange(move_count, dtype=jnp.int32)
    earlier = (counter[None, :] < counter[:, None]) & (targets[None, :] == targets[:, None])
    slot_index = targets * MOST + jnp.sum(earlier, axis=1)
    select = (jnp.arange(instances * MOST, dtype=jnp.int32)[:, None] == slot_index[None, :]).astype(
        jnp.bfloat16
    )
    picked = jnp.take(pool_pages, moved_ids, axis=0).reshape(move_count, -1)
    outgoing = jnp.dot(select, picked, preferred_element_type=jnp.float32).astype(jnp.bfloat16)
    outgoing = outgoing.reshape(instances, MOST, page_rows, 2, kv_width)
    occupied = (
        jnp.sum(select.astype(jnp.float32), axis=1).astype(jnp.bfloat16).reshape(instances, MOST)
    )
    incoming, arrived = (
        lax.all_to_all(outgoing, "ba", split_axis=0, concat_axis=0, tiled=True),
        lax.all_to_all(occupied, "ba", split_axis=0, concat_axis=0, tiled=True),
    )
    moved_rows = incoming.reshape(-1, 2, kv_width)
    moved_live = jnp.broadcast_to(
        (arrived > 0.5)[:, :, None], (instances, MOST, page_rows)
    ).reshape(-1)
    resident = jnp.take(pool_pages, page_table[0], axis=0).reshape(-1, 2, kv_width)
    resident_live = jnp.arange(resident.shape[0], dtype=jnp.int32) < ctx_len[0, 0]
    fresh_rows = new_kv[0]
    fresh_count = fresh_rows.shape[0]
    fresh_place = position * fresh_count + jnp.arange(fresh_count, dtype=jnp.int32)
    fresh_visible = fresh_place[None, :] <= jnp.arange(query_count, dtype=jnp.int32)[:, None]
    resident_visible = jnp.broadcast_to(
        resident_live[None, :], (query_count, resident_live.shape[0])
    )
    moved_visible = jnp.broadcast_to(moved_live[None, :], (query_count, moved_live.shape[0]))
    partials = attend_rows(
        query_heads,
        jnp.concatenate([resident, moved_rows, fresh_rows], axis=0),
        jnp.concatenate([resident_visible, moved_visible, fresh_visible], axis=1),
    )
    run_max, run_sum, run_out = partials
    top_max = lax.pmax(run_max, "aa")
    rescale = jnp.exp(run_max - top_max)
    numerator = (run_out * rescale[..., None]).reshape(query_count, -1, HEAD_DIM)
    denominator = (run_sum * rescale).reshape(query_count, -1)
    numerator, denominator = (
        lax.psum_scatter(numerator, "aa", scatter_dimension=1, tiled=True),
        lax.psum_scatter(denominator, "aa", scatter_dimension=1, tiled=True),
    )
    result = numerator / denominator[..., None]
    attended = result.reshape(1, query_count, -1).astype(jnp.bfloat16)
    zero = jnp.zeros((), jnp.int32)
    updated = lax.dynamic_update_slice(
        pool_pages, fresh_rows[None], (append_page[0, 0], zero, zero, zero)
    )
    return (attended, updated[None])


def solution(mesh):
    return jax.shard_map(
        local,
        mesh=mesh,
        in_specs=(
            P("ba", None, "aa"),
            P("ba", "aa", None, None),
            P("ba", "aa", None, None, None),
            P("ba", "aa"),
            P("ba", "aa"),
            P("ba", "aa"),
            P("ba", "aa"),
            P("ba", "aa"),
        ),
        out_specs=(P("ba", None, "aa"), P("ba", "aa", None, None, None)),
        check_vma=False,
    )
```

profile of v0, /device:TPU:0, one launch (start us, length us, event | category | flops | bytes accessed | tf_op | source)
XLA Modules:
  0.0 153.0 jit_solution(5487155029179787509)
XLA Ops:
  7.2 0.0 all-gather.3.cloned.1.call-start
  7.2 1.0 copy.69
  8.3 1.8 %copy.50 = bf16[1,128,1024]{1,2,0:T(8,128)(2,1)} copy(bf16[1,128,1024]{2,1,0:T(8,128)(2,1)} %param.8) | data formatting | bytes 524288 | tf_op args[0]
  10.0 0.0 all-gather.3.cloned.1.call-update
  10.1 0.9 convert_reduce_fusion
  11.0 0.7 fusion.19
  11.6 0.1 fusion.15
  11.7 0.7 all_to_all.12
  12.4 6.3 %all-to-all-start = ((bf16[4,1,2]{2,1,0:T(2,128)(2,1)}), bf16[4,1,2]{2,1,0:T(2,128)(2,1)S(1)}, u32[]{:S(2)}, u32[]{:S(2)}) async-start(bf16[4,1,2]{2,1,0:T(2,128)(2,1)} %all_to_all.12), calls=%async_computation | async-start | bytes 4096 | tf_op jit(solution)/shard_map/all_to_all | solution.py:87
  18.8 0.7 fusion.18
  19.4 0.9 gather_fusion.1
  20.4 0.1 gather.15
  20.5 0.7 compare_and_fusion
  21.2 0.4 convolution_convert_fusion
  21.6 0.4 reshape.150
  22.0 0.9 copy.45
  22.9 0.7 fusion.17
  23.5 1.1 gather_fusion
  24.6 0.2 reshape.174
  24.8 0.7 compare_and_fusion.1
  25.4 0.1 broadcast_in_dim.97
  25.5 0.1 broadcast_in_dim.98
  26.3 0.1 copy_select_fusion
  26.4 0.0 all-to-all-done
  26.4 5.1 %all-to-all-start.1 = ((bf16[4,2,32,2,512]{4,2,1,3,0:T(8,128)(2,1)}), bf16[4,2,32,2,512]{4,2,1,3,0:T(8,128)(2,1)S(1)}, u32[]{:S(2)}, u32[]{:S(2)}) async-start(bf16[4,2,32,2,512]{4,2,1,3,0:T(8,128)(2,1)} %copy.45), calls=%async_computation.1 | async-start | bytes 1048576 | tf_op jit(solution)/shard_map/all_to_all | solution.py:86
  31.5 0.0 reduce-scatter.2.cloned.1.call-start
  31.5 0.8 reshape.175
  32.3 0.1 iota_compare_fusion
  32.4 0.1 broadcast_in_dim.93
  32.5 0.1 reshape.178
  32.6 0.1 pad_add_fusion
  32.7 12.7 %all-to-all-done.1 = bf16[4,2,32,2,512]{4,2,1,3,0:T(8,128)(2,1)S(1)} async-done(((bf16[4,2,32,2,512]{4,2,1,3,0:T(8,128)(2,1)}), bf16[4,2,32,2,512]{4,2,1,3,0:T(8,128)(2,1)S(1)}, u32[]{:S(2)}, u32[]{:S(2)}) %all-to-all-start.1) | async-done | bytes 524320 | tf_op jit(solution)/shard_map/all_to_all | solution.py:86
  45.5 0.1 concatenate.12
  45.6 0.1 copy.48
  45.7 0.1 pad_maximum_fusion
  45.7 0.0 all-gather.3.cloned.1.call-done
  45.8 8.2 %fusion = (f32[128,4,16]{0,2,1:T(8,128)S(1)}, f32[4,400,128,16]{2,1,3,0:T(8,128)}) fusion(pred[128,400]{0,1:T(8,128)(4,1)S(1)} %pad_add_fusion, bf16[128,4,16,128]{0,3,2,1:T(8,128)(2,1)} %bitcast.71, bf16[400,2,4,128]{3,0,2,1:T(8,128)(2,1)S(1)} %pad_maximum_fusion), kind=kOutput, calls=%fused_computation.5 | convolution fusion | flops 848683008 | bytes 15697920 | tf_op jit(solution)/shard_map/while/body/eval_jaxpr/qkgd,rkd->qkgr/dot_general | solution.py:34
  53.9 23.4 %pmax.7 = f32[128,4,16]{0,2,1:T(8,128)S(1)} all-reduce(f32[128,4,16]{0,2,1:T(8,128)S(1)} %broadcast_maximum_fusion), channel_id=1, replica_groups=mesh['aa'=8,'ba'=4] {'aa'}, use_global_device_ids=true, to_apply=%region_3.4 | all-reduce | flops 8192 | bytes 65536 | tf_op jit(solution)/shard_map/pmax | solution.py:109
  77.3 0.0 copy-start
  77.3 8.3 %fusion.1 = f32[128,4,16]{0,2,1:T(8,128)S(1)} fusion(f32[4,400,128,16]{2,1,3,0:T(8,128)} %get-tuple-element.20, f32[128,4,16]{0,2,1:T(8,128)S(1)} %broadcast_maximum_fusion, pred[128,400]{0,1:T(8,128)(4,1)S(1)} %pad_add_fusion), kind=kLoop, calls=%fused_computation.6 | loop fusion | flops 16375808 | bytes 13223936 | tf_op jit(solution)/shard_map/while/body/eval_jaxpr/reduce_sum | solution.py:44
  85.7 0.1 copy-done
  85.8 0.0 copy-start.3
  85.8 0.0 copy-start.2
  85.8 9.8 %fusion.8 = f32[128,4,16,128]{0,3,2,1:T(8,128)} fusion(f32[4,400,128,16]{2,1,3,0:T(8,128)S(1)} %copy-done, f32[128,4,16]{0,2,1:T(8,128)S(1)} %broadcast_maximum_fusion, pred[128,400]{0,1:T(8,128)(4,1)S(1)} %pad_add_fusion, f32[128,4,16]{0,2,1:T(8,128)S(1)} %get-tuple-element.17, f32[128,4,16]{0,2,1:T(8,128)S(1)} %get-tuple-element.18, ...), kind=kOutput, calls=%fused_computation.14 | convolution fusion | flops 5048369152 | bytes 17860608 | tf_op jit(solution)/shard_map/while/body/eval_jaxpr/qkgr,rkd->qkgd/dot_general | solution.py:46
  95.5 0.0 reduce-scatter.2.cloned.1.call-update
  96.2 0.0 copy-done.3
  96.2 0.6 dynamic-slice.1
  97.5 0.0 copy-done.2
  97.5 0.0 copy-start.1
  97.5 22.6 %all-reduce = f32[128,64]{0,1:T(8,128)S(1)} all-reduce(f32[128,64]{0,1:T(8,128)S(1)} %bitcast.75), channel_id=4, replica_groups=mesh['aa'=8,'ba'=4] {'aa'}, use_global_device_ids=true, to_apply=%region_6.7.clone | all-reduce | flops 8192 | bytes 65536
  120.2 24.0 %reduce-scatter.2.cloned.1.call-done = f32[128,8,128]{0,2,1:T(8,128)} async-done(((f32[128,64,128]{0,2,1:T(8,128)}), f32[128,8,128]{0,2,1:T(8,128)}) %reduce-scatter.2.cloned.1.call-update) | async-done | bytes 524304 | tf_op jit(solution)/shard_map/reduce_scatter | solution.py:114
  144.2 1.1 divide_convert_fusion
  145.3 0.9 copy.60
  146.1 0.0 copy-done.1
  (13 shorter events, 0.2 us)
Async XLA Ops:
  7.2 38.6 %all-gather.3.cloned.1.call-start = ((), (), s32[]{:S(2)}) async-start(), calls=%async_computation.4 | async-start | bytes 2359296 | tf_op jit(solution)/shard_map/all_gather | solution.py:67
  12.4 14.0 %all-to-all-start = ((bf16[4,1,2]{2,1,0:T(2,128)(2,1)}), bf16[4,1,2]{2,1,0:T(2,128)(2,1)S(1)}, u32[]{:S(2)}, u32[]{:S(2)}) async-start(bf16[4,1,2]{2,1,0:T(2,128)(2,1)} %all_to_all.12), calls=%async_computation | async-start | bytes 4096 | tf_op jit(solution)/shard_map/all_to_all | solution.py:87
  26.4 19.0 %all-to-all-start.1 = ((bf16[4,2,32,2,512]{4,2,1,3,0:T(8,128)(2,1)}), bf16[4,2,32,2,512]{4,2,1,3,0:T(8,128)(2,1)S(1)}, u32[]{:S(2)}, u32[]{:S(2)}) async-start(bf16[4,2,32,2,512]{4,2,1,3,0:T(8,128)(2,1)} %copy.45), calls=%async_computation.1 | async-start | bytes 1048576 | tf_op jit(solution)/shard_map/all_to_all | solution.py:86
  31.5 112.7 %reduce-scatter.2.cloned.1.call-start = ((), (), s32[]{:S(2)}) async-start(), calls=%async_computation.3 | async-start | bytes 4718592 | tf_op jit(solution)/shard_map/reduce_scatter | solution.py:114
  77.3 8.5 %copy-start = (f32[4,400,128,16]{2,1,3,0:T(8,128)S(1)}, f32[4,400,128,16]{2,1,3,0:T(8,128)}, u32[]{:S(2)}) copy-start(f32[4,400,128,16]{2,1,3,0:T(8,128)} %get-tuple-element.20) | copy-start | bytes 39321604
  85.8 10.5 %copy-start.3 = (u32[32]{0:T(128)S(1)}, u32[32]{0:T(128)}, u32[]{:S(2)}) copy-start(u32[32]{0:T(128)} %constant.79) | copy-start | bytes 388
  85.8 11.7 %copy-start.2 = (bf16[1,16,2,512]{3,2,1,0:T(2,128)(2,1)S(1)}, bf16[1,16,2,512]{3,2,1,0:T(2,128)(2,1)}, u32[]{:S(2)}) copy-start(bf16[1,16,2,512]{3,2,1,0:T(2,128)(2,1)} %param.9) | copy-start | bytes 98308
  97.5 48.6 %copy-start.1 = (bf16[1,8,32,2,512]{4,3,2,1,0:T(2,128)(2,1)}, bf16[1,8,32,2,512]{4,3,2,1,0:T(2,128)(2,1)S(1)}, u32[]{:S(2)}) copy-start(bf16[1,8,32,2,512]{4,3,2,1,0:T(2,128)(2,1)S(1)} %bitcast_dynamic-update-slice_fusion) | copy-start | bytes 1572868
Sparse Core Ops, SparseCore 0:
  10.4 30.5 all-gather.2
  95.7 48.4 reduce-scatter.1
where the time goes:
time: 154 us; the launch traced here: 153 us
  blocking collectives  46 us (30%)
  waiting for transfers between devices  36.8 us (24%)
  matrix products  18.3 us (12%)
  between operations  16.2 us (11%)
  other arithmetic  14.2 us (9%)
  starting transfers between devices  11.5 us (7%)
  local copies, waits for them, and re-layouts  10 us (6%)
    reduce_scatter x1, waiting for transfers between devices, local(): lax.psum_scatter(numerator, 'aa', scatter_dimension=1, tiled=True)  24 us
    pmax x1, blocking collectives, local(): top_max = lax.pmax(run_max, 'aa')  23.4 us
    unnamed x1, blocking collectives  22.6 us
    all_to_all x1, waiting for transfers between devices, local(): lax.all_to_all(outgoing, 'ba', split_axis=0, concat_axis=0, tiled=True)  12.7 us
    dot_general x1, matrix products, block_step(): jnp.einsum('qkgr,rkd->qkgd', weights, block_values, precision=lax.Precisi...  9.77 us
    reduce_sum x1, other arithmetic, block_step(): new_sum = run_sum * shrink + jnp.sum(weights, axis=-1)  8.35 us
    dot_general x1, matrix products, block_step(): jnp.einsum('qkgd,rkd->qkgr', query_heads, block_keys[:, 0], preferred_ele...  8.16 us
    all_to_all x1, starting transfers between devices, local(): lax.all_to_all(occupied, 'ba', split_axis=0, concat_axis=0, tiled=True)  6.35 us
  transfers between devices with their start and end apart: 4, of which 2 were waited for; matrix products, arithmetic and copies ran while one was open for 7% of the time, Pallas kernels for 0%

commit v1 on v0

v1 whole, which is shorter than its diff:
```python
import functools
import math

import jax
import jax.numpy as jnp
from jax import lax
from jax.experimental import pallas as pl
from jax.experimental.pallas import tpu as pltpu
from jax.sharding import PartitionSpec as P

HEAD_DIM = 128
MOST = 2
LANES = 128
NEG_LARGE = -1e30
MESH = pl.DeviceIdType.MESH


def kernel(
    n_inst, n_aa, kv_heads,
    table_ref, len_ref, page_ref, dest_ref, q_ref, pages_ref, fresh_ref,
    out_ref,
    st_res, st_mov, st_len, st_occ,
    kv_res, kv_new, kv_mov, len_all, occ_all,
    run_max, run_sum, run_out,
    s_res, r_res, s_new, r_new, s_mov, r_mov, s_len, r_len, s_occ, r_occ,
    fs_res, fr_res, fs_new, fr_new, fs_mov, fr_mov, fs_len, fr_len, fs_occ, fr_occ,
    l_new, l_res,
):
    b = lax.axis_index("ba")
    a = lax.axis_index("aa")
    share = n_aa // kv_heads
    mine, member = a // share, a % share
    table = table_ref.shape[1]
    moves = page_ref.shape[1]
    page_rows = pages_ref.shape[3]
    queries = q_ref.shape[0]
    heads = q_ref.shape[1] // HEAD_DIM

    def inst(r):
        return lax.rem(b + r + n_inst, n_inst)

    def at_head(j):
        return lax.rem(mine + j + kv_heads, kv_heads) * share + member

    def peer(k):
        return mine * share + lax.rem(member + k + share, share)

    barrier = pltpu.get_barrier_semaphore()
    partners = [(r, j) for r in range(n_inst) for j in range(kv_heads) if r or j]
    for r, j in partners:
        pl.semaphore_signal(barrier, inc=1, device_id={"ba": inst(r), "aa": at_head(j)}, device_id_type=MESH)
    for k in range(1, share):
        pl.semaphore_signal(barrier, inc=1, device_id={"ba": b, "aa": peer(k)}, device_id_type=MESH)

    lane = lax.broadcasted_iota(jnp.int32, (8, LANES), 1)
    for r in range(1, n_inst):
        target = inst(r)
        slot_bias = []
        for m in range(MOST):
            chosen, occupied, seen = jnp.int32(0), jnp.int32(0), jnp.int32(0)
            for i in range(moves):
                hit = (dest_ref[0, i] == target).astype(jnp.int32)
                here = hit * (seen == m).astype(jnp.int32)
                chosen = chosen + here * page_ref[0, i]
                occupied = occupied + here
                seen = seen + hit
            st_mov[r - 1, :, :, m * page_rows:(m + 1) * page_rows, :] = pages_ref[chosen]
            slot_bias.append(jnp.where(occupied > 0, 0.0, NEG_LARGE))
        row = jnp.full((8, LANES), slot_bias[0], jnp.float32)
        for m in range(1, MOST):
            row = jnp.where((lane // page_rows) % MOST == m, slot_bias[m], row)
        st_occ[r - 1] = row
    for j in range(table):
        st_res[:, :, j * page_rows:(j + 1) * page_rows, :] = pages_ref[table_ref[0, j]]
    place = lax.broadcasted_iota(jnp.int32, st_len.shape, 1)
    st_len[...] = jnp.where(place < len_ref[0, 0], 0.0, NEG_LARGE)
    len_all[a] = st_len[...]

    pl.semaphore_wait(barrier, len(partners) + share - 1)

    def remote(src, dst, ss, rs, ba, aa):
        return pltpu.make_async_remote_copy(
            src_ref=src, dst_ref=dst, send_sem=ss, recv_sem=rs,
            device_id={"ba": ba, "aa": aa}, device_id_type=MESH,
        )

    sent = []

    def start(*args):
        c = remote(*args)
        c.start()
        sent.append(c)

    for r in range(1, n_inst):
        for j in range(kv_heads):
            to = at_head(j)
            h = lax.rem(mine + j, kv_heads)
            start(st_mov.at[r - 1, h], kv_mov.at[r - 1, a], s_mov.at[r - 1, j], r_mov.at[r - 1, j], inst(r), to)
            start(st_occ.at[r - 1], occ_all.at[r - 1, a], s_occ.at[r - 1, j], r_occ.at[r - 1, j], inst(r), to)
        if r == 1:
            for j in range(1, kv_heads):
                to = at_head(j)
                h = lax.rem(mine + j, kv_heads)
                start(fresh_ref.at[h], kv_new.at[a], s_new.at[j], r_new.at[j], b, to)
                start(st_len, len_all.at[a], s_len.at[j], r_len.at[j], b, to)
                start(st_res.at[h], kv_res.at[a], s_res.at[j], r_res.at[j], b, to)
            for k in range(1, share):
                to = peer(k)
                start(fresh_ref.at[mine], kv_new.at[a], fs_new.at[k - 1, 0], fr_new.at[k - 1, 0], b, to)
                start(st_len, len_all.at[a], fs_len.at[k - 1, 0], fr_len.at[k - 1, 0], b, to)
                start(st_res.at[mine], kv_res.at[a], fs_res.at[k - 1, 0], fr_res.at[k - 1, 0], b, to)
    own_new = pltpu.make_async_copy(fresh_ref.at[mine], kv_new.at[a], l_new)
    own_new.start()
    own_res = pltpu.make_async_copy(st_res.at[mine], kv_res.at[a], l_res)
    own_res.start()

    def arrived(slot, rs, ss):
        remote(slot, slot, ss, rs, b, a).wait_recv()

    def relay(slot, rs, ss, fs, fr, j):
        arrived(slot, rs, ss)
        for k in range(1, share):
            start(slot, slot, fs.at[k - 1, j], fr.at[k - 1, j], b, peer(k))

    def peers_done(buf, fs, fr, first=0):
        for k in range(1, share):
            for j in range(kv_heads):
                src = lax.rem(mine - j + kv_heads, kv_heads) * share + lax.rem(member - k + share, share)
                arrived(buf.at[src], fr.at[k - 1, j], fs.at[k - 1, j])

    for j in range(1, kv_heads):
        src = at_head(-j)
        relay(kv_new.at[src], r_new.at[j], s_new.at[j], fs_new, fr_new, j)
        relay(len_all.at[src], r_len.at[j], s_len.at[j], fs_len, fr_len, j)
        relay(kv_res.at[src], r_res.at[j], s_res.at[j], fs_res, fr_res, j)

    scale = math.log2(math.e) / math.sqrt(HEAD_DIM)

    def attend(keys, values, bias, first):
        def one_head(h, carry):
            q = q_ref[:, pl.ds(pl.multiple_of(h * HEAD_DIM, HEAD_DIM), HEAD_DIM)]
            s = lax.dot_general(q, keys(), (((1,), (1,)), ((), ())), preferred_element_type=jnp.float32)
            s = s * scale + bias
            top = jnp.max(s, axis=1, keepdims=True)
            if not first:
                old = run_max[h]
                top = jnp.maximum(old, top)
            w = jnp.exp2(s - top)
            total = jnp.sum(w, axis=1, keepdims=True)
            high = w.astype(jnp.bfloat16)
            low = (w - high.astype(jnp.float32)).astype(jnp.bfloat16)
            v = values()
            out = jnp.dot(high, v, preferred_element_type=jnp.float32)
            out = out + jnp.dot(low, v, preferred_element_type=jnp.float32)
            if not first:
                shrink = jnp.exp2(old - top)
                total = total + run_sum[h] * shrink
                out = out + run_out[h] * shrink
            run_max[h] = top
            run_sum[h] = total
            run_out[h] = out
            return carry
        lax.fori_loop(0, heads, one_head, 0)

    own_new.wait()
    peers_done(kv_new, fs_new, fr_new)
    rows = lax.broadcasted_iota(jnp.int32, (queries, queries), 0)
    columns = lax.broadcasted_iota(jnp.int32, (queries, queries), 1)
    attend(
        lambda: kv_new[:, 0].reshape(-1, HEAD_DIM),
        lambda: kv_new[:, 1].reshape(-1, HEAD_DIM),
        jnp.where(columns <= rows, 0.0, NEG_LARGE),
        True,
    )
    own_res.wait()
    peers_done(len_all, fs_len, fr_len)
    peers_done(kv_res, fs_res, fr_res)
    attend(
        lambda: kv_res[:, 0].reshape(-1, HEAD_DIM),
        lambda: kv_res[:, 1].reshape(-1, HEAD_DIM),
        jnp.concatenate([len_all[i, 0:1, :] for i in range(n_aa)], axis=1),
        False,
    )
    packed = LANES // (MOST * page_rows)
    lane1 = lax.broadcasted_iota(jnp.int32, (1, LANES), 1)
    for r in range(1, n_inst):
        for j in range(kv_heads):
            src = at_head(-j)
            relay(kv_mov.at[r - 1, src], r_mov.at[r - 1, j], s_mov.at[r - 1, j], fs_mov.at[r - 1], fr_mov.at[r - 1], j)
            relay(occ_all.at[r - 1, src], r_occ.at[r - 1, j], s_occ.at[r - 1, j], fs_occ.at[r - 1], fr_occ.at[r - 1], j)
        peers_done(kv_mov.at[r - 1], fs_mov.at[r - 1], fr_mov.at[r - 1])
        peers_done(occ_all.at[r - 1], fs_occ.at[r - 1], fr_occ.at[r - 1])
        pieces = []
        for g in range(n_aa // packed):
            piece = occ_all[r - 1, g * packed, 0:1, :]
            for i in range(1, packed):
                piece = jnp.where(lane1 >= i * MOST * page_rows, occ_all[r - 1, g * packed + i, 0:1, :], piece)
            pieces.append(piece)
        attend(
            lambda: kv_mov[r - 1, :, 0].reshape(-1, HEAD_DIM),
            lambda: kv_mov[r - 1, :, 1].reshape(-1, HEAD_DIM),
            jnp.concatenate(pieces, axis=1),
            False,
        )
    for h in range(heads):
        out_ref[:, h * HEAD_DIM:(h + 1) * HEAD_DIM] = (run_out[h] / run_sum[h]).astype(out_ref.dtype)
    for c in sent:
        c.wait_send()


def local(n_inst, n_aa, queries, new_kv, pool, page_table, ctx_len, move_page, move_dest, append_page):
    pool_pages = pool[0]
    pages, page_rows, _, width = pool_pages.shape
    kv_heads = width // HEAD_DIM
    share = n_aa // kv_heads
    fresh_rows = new_kv[0]
    fresh_count = fresh_rows.shape[0]
    split = pool_pages.reshape(pages, page_rows, 2, kv_heads, HEAD_DIM).transpose(0, 3, 2, 1, 4)
    fresh = fresh_rows.reshape(fresh_count, 2, kv_heads, HEAD_DIM).transpose(2, 1, 0, 3)
    query_count, q_width = queries.shape[1:]
    heads = q_width // HEAD_DIM
    table = page_table.shape[1]
    far = n_inst - 1
    bf, f32 = jnp.bfloat16, jnp.float32
    dma = pltpu.SemaphoreType.DMA
    near = [dma((kv_heads,))] * 4
    attended = pl.pallas_call(
        functools.partial(kernel, n_inst, n_aa, kv_heads),
        out_shape=jax.ShapeDtypeStruct((query_count, q_width), bf),
        in_specs=[pl.BlockSpec(memory_space=pltpu.SMEM)] * 4 + [pl.BlockSpec(memory_space=pltpu.VMEM)] * 3,
        out_specs=pl.BlockSpec(memory_space=pltpu.VMEM),
        scratch_shapes=[
            pltpu.VMEM((kv_heads, 2, table * page_rows, HEAD_DIM), bf),
            pltpu.VMEM((far, kv_heads, 2, MOST * page_rows, HEAD_DIM), bf),
            pltpu.VMEM((8, table * page_rows), f32),
            pltpu.VMEM((far, 8, LANES), f32),
            pltpu.VMEM((n_aa, 2, table * page_rows, HEAD_DIM), bf),
            pltpu.VMEM((n_aa, 2, fresh_count, HEAD_DIM), bf),
            pltpu.VMEM((far, n_aa, 2, MOST * page_rows, HEAD_DIM), bf),
            pltpu.VMEM((n_aa, 8, table * page_rows), f32),
            pltpu.VMEM((far, n_aa, 8, LANES), f32),
            pltpu.VMEM((heads, query_count, 1), f32),
            pltpu.VMEM((heads, query_count, 1), f32),
            pltpu.VMEM((heads, query_count, HEAD_DIM), f32),
            *near,
            dma((far, kv_heads)), dma((far, kv_heads)),
            dma((kv_heads,)), dma((kv_heads,)),
            dma((far, kv_heads)), dma((far, kv_heads)),
            *([dma((share - 1, kv_heads))] * 4),
            dma((far, share - 1, kv_heads)), dma((far, share - 1, kv_heads)),
            dma((share - 1, kv_heads)), dma((share - 1, kv_heads)),
            dma((far, share - 1, kv_heads)), dma((far, share - 1, kv_heads)),
            dma, dma,
        ],
        compiler_params=pltpu.CompilerParams(collective_id=0, has_side_effects=True),
        name="paged_attention",
    )(page_table, ctx_len, move_page, move_dest, queries[0], split, fresh)
    zero = jnp.zeros((), jnp.int32)
    updated = lax.dynamic_update_slice(pool_pages, fresh_rows[None], (append_page[0, 0], zero, zero, zero))
    return (attended[None], updated[None])


def solution(mesh):
    return jax.shard_map(
        functools.partial(local, mesh.shape["ba"], mesh.shape["aa"]),
        mesh=mesh,
        in_specs=(
            P("ba", None, "aa"),
            P("ba", "aa", None, None),
            P("ba", "aa", None, None, None),
            P("ba", "aa"),
            P("ba", "aa"),
            P("ba", "aa"),
            P("ba", "aa"),
            P("ba", "aa"),
        ),
        out_specs=(P("ba", None, "aa"), P("ba", "aa", None, None, None)),
        check_vma=False,
    )
```

time: 154 us -> 51.6 us (0.34)
  blocking collectives: 46 us -> 0 us
  Pallas kernels: 0 us -> 44.2 us
  waiting for transfers between devices: 36.8 us -> 0 us
  matrix products: 18.3 us -> 0 us
  between operations: 16.2 us -> 1.97 us
  other arithmetic: 14.2 us -> 0 us
  starting transfers between devices: 11.5 us -> 0 us
  local copies, waits for them, and re-layouts: 10 us -> 5.09 us
    pallas_call x0 -> x1, Pallas kernels: none -> 44.2 us  [local(): pl.pallas_call(functools.partial(kernel, n_inst, n_aa, kv_heads), out_sha...]
    reduce_scatter x1 -> x0, waiting for transfers between devices: 24 us -> none  [local(): lax.psum_scatter(numerator, 'aa', scatter_dimension=1, tiled=True)]
    pmax x1 -> x0, blocking collectives: 23.4 us -> none  [local(): top_max = lax.pmax(run_max, 'aa')]
    unnamed x1 -> x0, blocking collectives: 22.6 us -> none
    dot_general x3 -> x0, matrix products: 18.3 us -> none  [the longest x1 9.77 us: block_step(): jnp.einsum('qkgr,rkd->qkgd', weights, block_values, precision=lax.Precisi...]
    all_to_all x2 -> x0, waiting for transfers between devices: 12.7 us -> none  [the longest x1 12.7 us: local(): lax.all_to_all(outgoing, 'ba', split_axis=0, concat_axis=0, tiled=True)]
    all_to_all x2 -> x0, starting transfers between devices: 11.4 us -> none  [the longest x1 6.35 us: local(): lax.all_to_all(occupied, 'ba', split_axis=0, concat_axis=0, tiled=True)]
    reduce_sum x3 -> x0, other arithmetic: 9.35 us -> none  [the longest x1 8.35 us: block_step(): new_sum = run_sum * shrink + jnp.sum(weights, axis=-1)]
  transfers between devices with their start and end apart: 4 -> 0, of which waited for: 2 -> 0; matrix products, arithmetic and copies ran while one was open for 7% -> 0% of each run, Pallas kernels for 0% -> 0%
where the time goes in v1:
time: 51.6 us; the launch traced here: 51.3 us
  Pallas kernels  44.2 us (86%)
  local copies, waits for them, and re-layouts  5.09 us (10%)
  between operations  1.97 us (4%)
    pallas_call x1, Pallas kernels, local(): pl.pallas_call(functools.partial(kernel, n_inst, n_aa, kv_heads), out_sha...  44.2 us
    unnamed x6, local copies, waits for them, and re-layouts  3.13 us
    another operation x2, local copies, waits for them, and re-layouts, local(): pool_pages.reshape(pages, page_rows, 2, kv_heads, HEAD_DIM)  1.27 us

profile of v1, /device:TPU:0, one launch (start us, length us, event | category | flops | bytes accessed | tf_op | source)
XLA Modules:
  0.0 51.3 jit_solution(558797437824351410)
XLA Ops:
  0.6 1.0 %copy.27 = bf16[1,8,32,2,512]{4,3,2,1,0:T(2,128)(2,1)S(1)} copy(bf16[1,8,32,2,512]{4,3,2,1,0:T(2,128)(2,1)} %param.10) | data formatting | bytes 1048576
  2.3 0.0 copy-start.1
  2.3 0.3 reshape.7
  2.7 0.4 copy-done.1
  3.1 0.0 copy-start
  3.1 0.9 %copy.20 = bf16[8,32,2,4,128]{4,1,2,3,0:T(8,128)(2,1)} copy(bf16[8,32,2,4,128]{4,3,2,1,0:T(4,128)(2,1)S(1)} %reshape.7) | data formatting | bytes 1048576 | tf_op jit(solution)/shard_map/reshape;squeeze | solution.py:218
  4.1 0.0 copy-done
  4.1 0.6 %copy.21 = bf16[16,2,4,128]{3,0,1,2:T(8,128)(2,1)} copy(bf16[16,2,4,128]{3,2,1,0:T(4,128)(2,1)S(1)} %reshape.8) | data formatting | bytes 65536 | tf_op jit(solution)/shard_map/reshape;squeeze | solution.py:219
  5.4 44.2 %paged_attention.1 = bf16[128,1024]{1,0:T(8,128)(2,1)} custom-call(s32[1,4]{1,0:T(1,128)} %table_ref.1, s32[1,1]{1,0:T(1,128)S(6)} %copy.25.len_ref, s32[1,3]{1,0:T(1,128)} %page_ref.1, s32[1,3]{1,0:T(1,128)} %dest_ref.1, bf16[128,1024]{1,0:T(8,128)(2,1)} %bitcast.16, bf16[8,4,2,32,128]{4,3,2,1,0:T(8,128)(2,1)} %bitcast.14, bf16[4,2,16,128]{3,2,1,0:T(8,128)(2,1)} %bitcast.17), custom_call_target="tpu_custom_call" | custom-call | tf_op jit(solution)/shard_map/paged_attention/pallas_call | solution.py:227
  49.6 1.7 %copy.28 = bf16[1,128,1024]{2,1,0:T(8,128)(2,1)} copy(bf16[1,128,1024]{2,1,0:T(8,128)(2,1)} %bitcast.15) | data formatting | bytes 524288
  (2 shorter events, 0.1 us)
Async XLA Ops:
  2.3 0.8 %copy-start.1 = (bf16[1,16,2,512]{3,2,1,0:T(2,128)(2,1)S(1)}, bf16[1,16,2,512]{3,2,1,0:T(2,128)(2,1)}, u32[]{:S(2)}) copy-start(bf16[1,16,2,512]{3,2,1,0:T(2,128)(2,1)} %param.9) | copy-start | bytes 98308
  3.1 1.0 %copy-start = (bf16[1,8,32,2,512]{4,3,2,1,0:T(2,128)(2,1)}, bf16[1,8,32,2,512]{4,3,2,1,0:T(2,128)(2,1)S(1)}, u32[]{:S(2)}) copy-start(bf16[1,8,32,2,512]{4,3,2,1,0:T(2,128)(2,1)S(1)} %bitcast_dynamic-update-slice_fusion) | copy-start | bytes 1572868

commit v2 on v1

--- a/solution.py
+++ b/solution.py
@@ -11,6 +11,7 @@
 HEAD_DIM = 128
 MOST = 2
 LANES = 128
+BLOCK = 256
 NEG_LARGE = -1e30
 MESH = pl.DeviceIdType.MESH
 
@@ -21,7 +22,7 @@
     out_ref,
     st_res, st_mov, st_len, st_occ,
     kv_res, kv_new, kv_mov, len_all, occ_all,
-    run_max, run_sum, run_out,
+    run_max, run_sum, run_out, q_turned,
     s_res, r_res, s_new, r_new, s_mov, r_mov, s_len, r_len, s_occ, r_occ,
     fs_res, fr_res, fs_new, fr_new, fs_mov, fr_mov, fs_len, fr_len, fs_occ, fr_occ,
     l_new, l_res,
@@ -52,7 +53,7 @@
     for k in range(1, share):
         pl.semaphore_signal(barrier, inc=1, device_id={"ba": b, "aa": peer(k)}, device_id_type=MESH)
 
-    lane = lax.broadcasted_iota(jnp.int32, (8, LANES), 1)
+    line = lax.broadcasted_iota(jnp.int32, (8, LANES), 0)
     for r in range(1, n_inst):
         target = inst(r)
         slot_bias = []
@@ -68,13 +69,14 @@
             slot_bias.append(jnp.where(occupied > 0, 0.0, NEG_LARGE))
         row = jnp.full((8, LANES), slot_bias[0], jnp.float32)
         for m in range(1, MOST):
-            row = jnp.where((lane // page_rows) % MOST == m, slot_bias[m], row)
+            row = jnp.where(line == m, slot_bias[m], row)
         st_occ[r - 1] = row
     for j in range(table):
         st_res[:, :, j * page_rows:(j + 1) * page_rows, :] = pages_ref[table_ref[0, j]]
-    place = lax.broadcasted_iota(jnp.int32, st_len.shape, 1)
-    st_len[...] = jnp.where(place < len_ref[0, 0], 0.0, NEG_LARGE)
+    st_len[...] = jnp.full(st_len.shape, len_ref[0, 0], jnp.int32)
     len_all[a] = st_len[...]
+    for h in range(heads):
+        q_turned[:, h * queries:(h + 1) * queries] = q_ref[:, h * HEAD_DIM:(h + 1) * HEAD_DIM].T
 
     pl.semaphore_wait(barrier, len(partners) + share - 1)
 
@@ -137,52 +139,51 @@
     scale = math.log2(math.e) / math.sqrt(HEAD_DIM)
 
     def attend(keys, values, bias, first):
-        def one_head(h, carry):
-            q = q_ref[:, pl.ds(pl.multiple_of(h * HEAD_DIM, HEAD_DIM), HEAD_DIM)]
-            s = lax.dot_general(q, keys(), (((1,), (1,)), ((), ())), preferred_element_type=jnp.float32)
-            s = s * scale + bias
-            top = jnp.max(s, axis=1, keepdims=True)
+        turned = values.T
+        copies = BLOCK // bias.shape[1]
+        wide = jnp.concatenate([bias] * copies, axis=1) if copies > 1 else bias
+        for start_at in range(0, heads * queries, BLOCK):
+            block = slice(start_at, start_at + BLOCK)
+            s = jnp.dot(keys, q_turned[:, block], preferred_element_type=jnp.float32)
+            s = s * scale + wide
+            top = jnp.max(s, axis=0, keepdims=True)
             if not first:
-                old = run_max[h]
+                old = run_max[:, block]
                 top = jnp.maximum(old, top)
             w = jnp.exp2(s - top)
-            total = jnp.sum(w, axis=1, keepdims=True)
+            total = jnp.sum(w, axis=0, keepdims=True)
             high = w.astype(jnp.bfloat16)
             low = (w - high.astype(jnp.float32)).astype(jnp.bfloat16)
-            v = values()
-            out = jnp.dot(high, v, preferred_element_type=jnp.float32)
-            out = out + jnp.dot(low, v, preferred_element_type=jnp.float32)
+            out = jnp.dot(turned, high, preferred_element_type=jnp.float32)
+            out = out + jnp.dot(turned, low, preferred_element_type=jnp.float32)
             if not first:
                 shrink = jnp.exp2(old - top)
-                total = total + run_sum[h] * shrink
-                out = out + run_out[h] * shrink
-            run_max[h] = top
-            run_sum[h] = total
-            run_out[h] = out
-            return carry
-        lax.fori_loop(0, heads, one_head, 0)
+                total = total + run_sum[:, block] * shrink
+                out = out + run_out[:, block] * shrink
+            run_max[:, block] = top
+            run_sum[:, block] = total
+            run_out[:, block] = out
 
     own_new.wait()
     peers_done(kv_new, fs_new, fr_new)
     rows = lax.broadcasted_iota(jnp.int32, (queries, queries), 0)
     columns = lax.broadcasted_iota(jnp.int32, (queries, queries), 1)
     attend(
-        lambda: kv_new[:, 0].reshape(-1, HEAD_DIM),
-        lambda: kv_new[:, 1].reshape(-1, HEAD_DIM),
-        jnp.where(columns <= rows, 0.0, NEG_LARGE),
+        kv_new[:, 0].reshape(-1, HEAD_DIM),
+        kv_new[:, 1].reshape(-1, HEAD_DIM),
+        jnp.where(rows <= columns, 0.0, NEG_LARGE),
         True,
     )
     own_res.wait()
+    place = lax.broadcasted_iota(jnp.int32, (table * page_rows, LANES), 0)
     peers_done(len_all, fs_len, fr_len)
     peers_done(kv_res, fs_res, fr_res)
     attend(
-        lambda: kv_res[:, 0].reshape(-1, HEAD_DIM),
-        lambda: kv_res[:, 1].reshape(-1, HEAD_DIM),
-        jnp.concatenate([len_all[i, 0:1, :] for i in range(n_aa)], axis=1),
+        kv_res[:, 0].reshape(-1, HEAD_DIM),
+        kv_res[:, 1].reshape(-1, HEAD_DIM),
+        jnp.concatenate([jnp.where(place < len_all[i, 0:1, :], 0.0, NEG_LARGE) for i in range(n_aa)], axis=0),
         False,
     )
-    packed = LANES // (MOST * page_rows)
-    lane1 = lax.broadcasted_iota(jnp.int32, (1, LANES), 1)
     for r in range(1, n_inst):
         for j in range(kv_heads):
             src = at_head(-j)
@@ -190,20 +191,22 @@
             relay(occ_all.at[r - 1, src], r_occ.at[r - 1, j], s_occ.at[r - 1, j], fs_occ.at[r - 1], fr_occ.at[r - 1], j)
         peers_done(kv_mov.at[r - 1], fs_mov.at[r - 1], fr_mov.at[r - 1])
         peers_done(occ_all.at[r - 1], fs_occ.at[r - 1], fr_occ.at[r - 1])
-        pieces = []
-        for g in range(n_aa // packed):
-            piece = occ_all[r - 1, g * packed, 0:1, :]
-            for i in range(1, packed):
-                piece = jnp.where(lane1 >= i * MOST * page_rows, occ_all[r - 1, g * packed + i, 0:1, :], piece)
-            pieces.append(piece)
+        pieces = [
+            jnp.broadcast_to(occ_all[r - 1, i, m:m + 1, :], (page_rows, LANES))
+            for i in range(n_aa) for m in range(MOST)
+        ]
         attend(
-            lambda: kv_mov[r - 1, :, 0].reshape(-1, HEAD_DIM),
-            lambda: kv_mov[r - 1, :, 1].reshape(-1, HEAD_DIM),
-            jnp.concatenate(pieces, axis=1),
+            kv_mov[r - 1, :, 0].reshape(-1, HEAD_DIM),
+            kv_mov[r - 1, :, 1].reshape(-1, HEAD_DIM),
+            jnp.concatenate(pieces, axis=0),
             False,
         )
+    def turn(h):
+        part = slice(h * queries, (h + 1) * queries)
+        return (run_out[:, part] / run_sum[:, part]).T
+
     for h in range(heads):
-        out_ref[:, h * HEAD_DIM:(h + 1) * HEAD_DIM] = (run_out[h] / run_sum[h]).astype(out_ref.dtype)
+        out_ref[:, h * HEAD_DIM:(h + 1) * HEAD_DIM] = turn(h).astype(out_ref.dtype)
     for c in sent:
         c.wait_send()
 
@@ -232,16 +235,17 @@
         scratch_shapes=[
             pltpu.VMEM((kv_heads, 2, table * page_rows, HEAD_DIM), bf),
             pltpu.VMEM((far, kv_heads, 2, MOST * page_rows, HEAD_DIM), bf),
-            pltpu.VMEM((8, table * page_rows), f32),
+            pltpu.VMEM((8, LANES), jnp.int32),
             pltpu.VMEM((far, 8, LANES), f32),
             pltpu.VMEM((n_aa, 2, table * page_rows, HEAD_DIM), bf),
             pltpu.VMEM((n_aa, 2, fresh_count, HEAD_DIM), bf),
             pltpu.VMEM((far, n_aa, 2, MOST * page_rows, HEAD_DIM), bf),
-            pltpu.VMEM((n_aa, 8, table * page_rows), f32),
+            pltpu.VMEM((n_aa, 8, LANES), jnp.int32),
             pltpu.VMEM((far, n_aa, 8, LANES), f32),
-            pltpu.VMEM((heads, query_count, 1), f32),
-            pltpu.VMEM((heads, query_count, 1), f32),
-            pltpu.VMEM((heads, query_count, HEAD_DIM), f32),
+            pltpu.VMEM((1, heads * query_count), f32),
+            pltpu.VMEM((1, heads * query_count), f32),
+            pltpu.VMEM((HEAD_DIM, heads * query_count), f32),
+            pltpu.VMEM((HEAD_DIM, heads * query_count), bf),
             *near,
             dma((far, kv_heads)), dma((far, kv_heads)),
             dma((kv_heads,)), dma((kv_heads,)),

time: 51.6 us -> 36.5 us (0.71)
  Pallas kernels: 44.2 us -> 29.2 us
    pallas_call x1, Pallas kernels: 44.2 us -> 29.2 us  [local(): pl.pallas_call(functools.partial(kernel, n_inst, n_aa, kv_heads), out_sha...]
where the time goes in v2:
time: 36.5 us; the launch traced here: 36.2 us
  Pallas kernels  29.2 us (80%)
  local copies, waits for them, and re-layouts  5.09 us (14%)
  between operations  1.97 us (5%)
    pallas_call x1, Pallas kernels, local(): pl.pallas_call(functools.partial(kernel, n_inst, n_aa, kv_heads), out_sha...  29.2 us
    unnamed x6, local copies, waits for them, and re-layouts  3.13 us
    another operation x2, local copies, waits for them, and re-layouts, local(): pool_pages.reshape(pages, page_rows, 2, kv_heads, HEAD_DIM)  1.27 us

profile of v2, /device:TPU:0, one launch (start us, length us, event | category | flops | bytes accessed | tf_op | source)
XLA Modules:
  0.0 36.2 jit_solution(791556912005929524)
XLA Ops:
  0.6 1.0 %copy.27 = bf16[1,8,32,2,512]{4,3,2,1,0:T(2,128)(2,1)S(1)} copy(bf16[1,8,32,2,512]{4,3,2,1,0:T(2,128)(2,1)} %param.10) | data formatting | bytes 1048576
  2.3 0.0 copy-start.1
  2.3 0.3 reshape.7
  2.7 0.4 %copy-done.1 = bf16[1,16,2,512]{3,2,1,0:T(2,128)(2,1)S(1)} copy-done((bf16[1,16,2,512]{3,2,1,0:T(2,128)(2,1)S(1)}, bf16[1,16,2,512]{3,2,1,0:T(2,128)(2,1)}, u32[]{:S(2)}) %copy-start.1) | copy-done | bytes 32792
  3.1 0.0 copy-start
  3.1 0.9 %copy.20 = bf16[8,32,2,4,128]{4,1,2,3,0:T(8,128)(2,1)} copy(bf16[8,32,2,4,128]{4,3,2,1,0:T(4,128)(2,1)S(1)} %reshape.7) | data formatting | bytes 1048576 | tf_op jit(solution)/shard_map/reshape;squeeze | solution.py:221
  4.1 0.0 copy-done
  4.1 0.6 %copy.21 = bf16[16,2,4,128]{3,0,1,2:T(8,128)(2,1)} copy(bf16[16,2,4,128]{3,2,1,0:T(4,128)(2,1)S(1)} %reshape.8) | data formatting | bytes 65536 | tf_op jit(solution)/shard_map/reshape;squeeze | solution.py:222
  5.4 29.2 %paged_attention.1 = bf16[128,1024]{1,0:T(8,128)(2,1)} custom-call(s32[1,4]{1,0:T(1,128)} %table_ref.1, s32[1,1]{1,0:T(1,128)S(6)} %copy.25.len_ref, s32[1,3]{1,0:T(1,128)} %page_ref.1, s32[1,3]{1,0:T(1,128)} %dest_ref.1, bf16[128,1024]{1,0:T(8,128)(2,1)} %bitcast.16, bf16[8,4,2,32,128]{4,3,2,1,0:T(8,128)(2,1)} %bitcast.14, bf16[4,2,16,128]{3,2,1,0:T(8,128)(2,1)} %bitcast.17), custom_call_target="tpu_custom_call" | custom-call | tf_op jit(solution)/shard_map/paged_attention/pallas_call | solution.py:230
  34.6 1.7 %copy.28 = bf16[1,128,1024]{2,1,0:T(8,128)(2,1)} copy(bf16[1,128,1024]{2,1,0:T(8,128)(2,1)} %bitcast.15) | data formatting | bytes 524288
  (2 shorter events, 0.1 us)
Async XLA Ops:
  2.3 0.8 %copy-start.1 = (bf16[1,16,2,512]{3,2,1,0:T(2,128)(2,1)S(1)}, bf16[1,16,2,512]{3,2,1,0:T(2,128)(2,1)}, u32[]{:S(2)}) copy-start(bf16[1,16,2,512]{3,2,1,0:T(2,128)(2,1)} %param.9) | copy-start | bytes 98308
  3.1 1.0 %copy-start = (bf16[1,8,32,2,512]{4,3,2,1,0:T(2,128)(2,1)}, bf16[1,8,32,2,512]{4,3,2,1,0:T(2,128)(2,1)S(1)}, u32[]{:S(2)}) copy-start(bf16[1,8,32,2,512]{4,3,2,1,0:T(2,128)(2,1)S(1)} %bitcast_dynamic-update-slice_fusion) | copy-start | bytes 1572868

commit v3 on v2

--- a/solution.py
+++ b/solution.py
@@ -18,9 +18,9 @@
 
 def kernel(
     n_inst, n_aa, kv_heads,
-    table_ref, len_ref, page_ref, dest_ref, q_ref, pages_ref, fresh_ref,
+    table_ref, len_ref, page_ref, dest_ref, q_ref, pool_ref, fresh_ref,
     out_ref,
-    st_res, st_mov, st_len, st_occ,
+    st_res, st_new, st_mov, st_len, st_occ,
     kv_res, kv_new, kv_mov, len_all, occ_all,
     run_max, run_sum, run_out, q_turned,
     s_res, r_res, s_new, r_new, s_mov, r_mov, s_len, r_len, s_occ, r_occ,
@@ -33,7 +33,7 @@
     mine, member = a // share, a % share
     table = table_ref.shape[1]
     moves = page_ref.shape[1]
-    page_rows = pages_ref.shape[3]
+    page_rows = pool_ref.shape[1]
     queries = q_ref.shape[0]
     heads = q_ref.shape[1] // HEAD_DIM
 
@@ -52,6 +52,11 @@
         pl.semaphore_signal(barrier, inc=1, device_id={"ba": inst(r), "aa": at_head(j)}, device_id_type=MESH)
     for k in range(1, share):
         pl.semaphore_signal(barrier, inc=1, device_id={"ba": b, "aa": peer(k)}, device_id_type=MESH)
+
+    spots = [(h, w) for h in range(kv_heads) for w in range(2)]
+
+    def columns_of(h):
+        return slice(h * HEAD_DIM, (h + 1) * HEAD_DIM)
 
     line = lax.broadcasted_iota(jnp.int32, (8, LANES), 0)
     for r in range(1, n_inst):
@@ -65,14 +70,18 @@
                 chosen = chosen + here * page_ref[0, i]
                 occupied = occupied + here
                 seen = seen + hit
-            st_mov[r - 1, :, :, m * page_rows:(m + 1) * page_rows, :] = pages_ref[chosen]
+            for h, w in spots:
+                st_mov[r - 1, h, w, m * page_rows:(m + 1) * page_rows, :] = pool_ref[chosen, :, w, columns_of(h)]
             slot_bias.append(jnp.where(occupied > 0, 0.0, NEG_LARGE))
         row = jnp.full((8, LANES), slot_bias[0], jnp.float32)
         for m in range(1, MOST):
             row = jnp.where(line == m, slot_bias[m], row)
         st_occ[r - 1] = row
     for j in range(table):
-        st_res[:, :, j * page_rows:(j + 1) * page_rows, :] = pages_ref[table_ref[0, j]]
+        for h, w in spots:
+            st_res[h, w, j * page_rows:(j + 1) * page_rows, :] = pool_ref[table_ref[0, j], :, w, columns_of(h)]
+    for h, w in spots:
+        st_new[h, w] = fresh_ref[:, w, columns_of(h)]
     st_len[...] = jnp.full(st_len.shape, len_ref[0, 0], jnp.int32)
     len_all[a] = st_len[...]
     for h in range(heads):
@@ -97,21 +106,21 @@
         for j in range(kv_heads):
             to = at_head(j)
             h = lax.rem(mine + j, kv_heads)
-            start(st_mov.at[r - 1, h], kv_mov.at[r - 1, a], s_mov.at[r - 1, j], r_mov.at[r - 1, j], inst(r), to)
-            start(st_occ.at[r - 1], occ_all.at[r - 1, a], s_occ.at[r - 1, j], r_occ.at[r - 1, j], inst(r), to)
+            start(st_mov.at[r - 1, h], kv_mov.at[r - 1, member, mine], s_mov.at[r - 1, j], r_mov.at[r - 1, j], inst(r), to)
+            start(st_occ.at[r - 1], occ_all.at[r - 1, member, mine], s_occ.at[r - 1, j], r_occ.at[r - 1, j], inst(r), to)
         if r == 1:
             for j in range(1, kv_heads):
                 to = at_head(j)
                 h = lax.rem(mine + j, kv_heads)
-                start(fresh_ref.at[h], kv_new.at[a], s_new.at[j], r_new.at[j], b, to)
+                start(st_new.at[h], kv_new.at[a], s_new.at[j], r_new.at[j], b, to)
                 start(st_len, len_all.at[a], s_len.at[j], r_len.at[j], b, to)
                 start(st_res.at[h], kv_res.at[a], s_res.at[j], r_res.at[j], b, to)
             for k in range(1, share):
                 to = peer(k)
-                start(fresh_ref.at[mine], kv_new.at[a], fs_new.at[k - 1, 0], fr_new.at[k - 1, 0], b, to)
+                start(st_new.at[mine], kv_new.at[a], fs_new.at[k - 1, 0], fr_new.at[k - 1, 0], b, to)
                 start(st_len, len_all.at[a], fs_len.at[k - 1, 0], fr_len.at[k - 1, 0], b, to)
                 start(st_res.at[mine], kv_res.at[a], fs_res.at[k - 1, 0], fr_res.at[k - 1, 0], b, to)
-    own_new = pltpu.make_async_copy(fresh_ref.at[mine], kv_new.at[a], l_new)
+    own_new = pltpu.make_async_copy(st_new.at[mine], kv_new.at[a], l_new)
     own_new.start()
     own_res = pltpu.make_async_copy(st_res.at[mine], kv_res.at[a], l_res)
     own_res.start()
@@ -178,29 +187,58 @@
     place = lax.broadcasted_iota(jnp.int32, (table * page_rows, LANES), 0)
     peers_done(len_all, fs_len, fr_len)
     peers_done(kv_res, fs_res, fr_res)
-    attend(
-        kv_res[:, 0].reshape(-1, HEAD_DIM),
-        kv_res[:, 1].reshape(-1, HEAD_DIM),
-        jnp.concatenate([jnp.where(place < len_all[i, 0:1, :], 0.0, NEG_LARGE) for i in range(n_aa)], axis=0),
-        False,
-    )
-    for r in range(1, n_inst):
-        for j in range(kv_heads):
-            src = at_head(-j)
-            relay(kv_mov.at[r - 1, src], r_mov.at[r - 1, j], s_mov.at[r - 1, j], fs_mov.at[r - 1], fr_mov.at[r - 1], j)
-            relay(occ_all.at[r - 1, src], r_occ.at[r - 1, j], s_occ.at[r - 1, j], fs_occ.at[r - 1], fr_occ.at[r - 1], j)
-        peers_done(kv_mov.at[r - 1], fs_mov.at[r - 1], fr_mov.at[r - 1])
-        peers_done(occ_all.at[r - 1], fs_occ.at[r - 1], fr_occ.at[r - 1])
-        pieces = [
-            jnp.broadcast_to(occ_all[r - 1, i, m:m + 1, :], (page_rows, LANES))
-            for i in range(n_aa) for m in range(MOST)
-        ]
+    def attend_resident():
         attend(
-            kv_mov[r - 1, :, 0].reshape(-1, HEAD_DIM),
-            kv_mov[r - 1, :, 1].reshape(-1, HEAD_DIM),
-            jnp.concatenate(pieces, axis=0),
+            kv_res[:, 0].reshape(-1, HEAD_DIM),
+            kv_res[:, 1].reshape(-1, HEAD_DIM),
+            jnp.concatenate([jnp.where(place < len_all[i, 0:1, :], 0.0, NEG_LARGE) for i in range(n_aa)], axis=0),
             False,
         )
+
+    far = n_inst - 1
+
+    def back(j):
+        return lax.rem(mine - j + kv_heads, kv_heads)
+
+    def other(k):
+        return lax.rem(member - k + share, share)
+
+    def relay_moved(r):
+        for j in range(kv_heads):
+            relay(kv_mov.at[r - 1, member, back(j)], r_mov.at[r - 1, j], s_mov.at[r - 1, j], fs_mov.at[r - 1], fr_mov.at[r - 1], j)
+            relay(occ_all.at[r - 1, member, back(j)], r_occ.at[r - 1, j], s_occ.at[r - 1, j], fs_occ.at[r - 1], fr_occ.at[r - 1], j)
+
+    def moved_from(r, k):
+        for j in range(kv_heads):
+            arrived(kv_mov.at[r - 1, other(k), back(j)], fr_mov.at[r - 1, k - 1, j], fs_mov.at[r - 1, k - 1, j])
+            arrived(occ_all.at[r - 1, other(k), back(j)], fr_occ.at[r - 1, k - 1, j], fs_occ.at[r - 1, k - 1, j])
+
+    def attend_moved(r, members):
+        attend(
+            jnp.concatenate([kv_mov[r - 1, i, :, 0].reshape(-1, HEAD_DIM) for i in members], axis=0),
+            jnp.concatenate([kv_mov[r - 1, i, :, 1].reshape(-1, HEAD_DIM) for i in members], axis=0),
+            jnp.concatenate([
+                jnp.broadcast_to(occ_all[r - 1, i, c, m:m + 1, :], (page_rows, LANES))
+                for i in members for c in range(kv_heads) for m in range(MOST)
+            ], axis=0),
+            False,
+        )
+
+    relay_moved(1)
+    attend_resident()
+    for r in range(1, far):
+        if r + 1 < far:
+            relay_moved(r + 1)
+        for k in range(1, share):
+            moved_from(r, k)
+        attend_moved(r, range(share))
+    if far > 1:
+        relay_moved(far)
+    attend_moved(far, [member])
+    for k in range(1, share):
+        moved_from(far, k)
+        attend_moved(far, [other(k)])
+
     def turn(h):
         part = slice(h * queries, (h + 1) * queries)
         return (run_out[:, part] / run_sum[:, part]).T
@@ -218,8 +256,6 @@
     share = n_aa // kv_heads
     fresh_rows = new_kv[0]
     fresh_count = fresh_rows.shape[0]
-    split = pool_pages.reshape(pages, page_rows, 2, kv_heads, HEAD_DIM).transpose(0, 3, 2, 1, 4)
-    fresh = fresh_rows.reshape(fresh_count, 2, kv_heads, HEAD_DIM).transpose(2, 1, 0, 3)
     query_count, q_width = queries.shape[1:]
     heads = q_width // HEAD_DIM
     table = page_table.shape[1]
@@ -234,14 +270,15 @@
         out_specs=pl.BlockSpec(memory_space=pltpu.VMEM),
         scratch_shapes=[
             pltpu.VMEM((kv_heads, 2, table * page_rows, HEAD_DIM), bf),
+            pltpu.VMEM((kv_heads, 2, fresh_count, HEAD_DIM), bf),
             pltpu.VMEM((far, kv_heads, 2, MOST * page_rows, HEAD_DIM), bf),
             pltpu.VMEM((8, LANES), jnp.int32),
             pltpu.VMEM((far, 8, LANES), f32),
             pltpu.VMEM((n_aa, 2, table * page_rows, HEAD_DIM), bf),
             pltpu.VMEM((n_aa, 2, fresh_count, HEAD_DIM), bf),
-            pltpu.VMEM((far, n_aa, 2, MOST * page_rows, HEAD_DIM), bf),
+            pltpu.VMEM((far, share, kv_heads, 2, MOST * page_rows, HEAD_DIM), bf),
             pltpu.VMEM((n_aa, 8, LANES), jnp.int32),
-            pltpu.VMEM((far, n_aa, 8, LANES), f32),
+            pltpu.VMEM((far, share, kv_heads, 8, LANES), f32),
             pltpu.VMEM((1, heads * query_count), f32),
             pltpu.VMEM((1, heads * query_count), f32),
             pltpu.VMEM((HEAD_DIM, heads * query_count), f32),
@@ -258,7 +295,7 @@
         ],
         compiler_params=pltpu.CompilerParams(collective_id=0, has_side_effects=True),
         name="paged_attention",
-    )(page_table, ctx_len, move_page, move_dest, queries[0], split, fresh)
+    )(page_table, ctx_len, move_page, move_dest, queries[0], pool_pages, fresh_rows)
     zero = jnp.zeros((), jnp.int32)
     updated = lax.dynamic_update_slice(pool_pages, fresh_rows[None], (append_page[0, 0], zero, zero, zero))
     return (attended[None], updated[None])

time: 36.5 us -> 33.5 us (0.918)
  Pallas kernels: 29.2 us -> 26.8 us
  local copies, waits for them, and re-layouts: 5.09 us -> 4.52 us
    pallas_call x1, Pallas kernels: 29.2 us -> 26.8 us  [local(): pl.pallas_call(functools.partial(kernel, n_inst, n_aa, kv_heads), out_sha...]
    another operation x4 -> x0, local copies, waits for them, and re-layouts: 1.92 us -> none  [the longest x2 1.27 us: local(): pool_pages.reshape(pages, page_rows, 2, kv_heads, HEAD_DIM)]
    unnamed x6 -> x4, local copies, waits for them, and re-layouts: 3.13 us -> 3.87 us
    dynamic_update_slice x1, local copies, waits for them, and re-layouts: 0.03 us -> 0.64 us  [local(): lax.dynamic_update_slice(pool_pages, fresh_rows[None], (append_page[0, 0]...]
where the time goes in v3:
time: 33.5 us; the launch traced here: 33.3 us
  Pallas kernels  26.8 us (80%)
  local copies, waits for them, and re-layouts  4.52 us (13%)
  between operations  1.96 us (6%)
    pallas_call x1, Pallas kernels, local(): pl.pallas_call(functools.partial(kernel, n_inst, n_aa, kv_heads), out_sha...  26.8 us
    unnamed x4, local copies, waits for them, and re-layouts  3.87 us

profile of v3, /device:TPU:0, one launch (start us, length us, event | category | flops | bytes accessed | tf_op | source)
XLA Modules:
  0.0 33.3 jit_solution(17236243860882500175)
XLA Ops:
  0.6 2.2 %copy.15 = bf16[1,8,32,2,512]{4,3,2,1,0:T(2,128)(2,1)} copy(bf16[1,8,32,2,512]{4,3,2,1,0:T(2,128)(2,1)} %param.10) | data formatting | bytes 1048576
  4.1 0.0 copy-start
  4.1 26.8 %paged_attention.1 = bf16[128,1024]{1,0:T(8,128)(2,1)} custom-call(s32[1,4]{1,0:T(1,128)} %table_ref.1, s32[1,1]{1,0:T(1,128)S(6)} %copy.13.len_ref, s32[1,3]{1,0:T(1,128)} %page_ref.1, s32[1,3]{1,0:T(1,128)} %dest_ref.1, bf16[128,1024]{1,0:T(8,128)(2,1)} %bitcast.12, bf16[8,32,2,512]{3,2,1,0:T(2,128)(2,1)} %bitcast.10, bf16[16,2,512]{2,1,0:T(2,128)(2,1)} %bitcast.13), custom_call_target="tpu_custom_call" | custom-call | tf_op jit(solution)/shard_map/paged_attention/pallas_call | solution.py:266
  30.9 0.0 copy-done
  30.9 0.6 %bitcast_dynamic-update-slice_fusion = bf16[1,8,32,2,512]{4,3,2,1,0:T(2,128)(2,1)} fusion(bf16[1,8,32,2,512]{4,3,2,1,0:T(2,128)(2,1)} %copy.15, s32[]{:T(128)S(6)} %select_n.3, bf16[1,16,2,512]{3,2,1,0:T(2,128)(2,1)S(1)} %copy-done), kind=kLoop, calls=%fused_computation | loop fusion | bytes 65540 | tf_op jit(solution)/shard_map/dynamic_update_slice | solution.py:300
  31.6 1.7 %copy.16 = bf16[1,128,1024]{2,1,0:T(8,128)(2,1)} copy(bf16[1,128,1024]{2,1,0:T(8,128)(2,1)} %bitcast.11) | data formatting | bytes 524288
Async XLA Ops:
  4.1 26.8 %copy-start = (bf16[1,16,2,512]{3,2,1,0:T(2,128)(2,1)S(1)}, bf16[1,16,2,512]{3,2,1,0:T(2,128)(2,1)}, u32[]{:S(2)}) copy-start(bf16[1,16,2,512]{3,2,1,0:T(2,128)(2,1)} %param.9) | copy-start | bytes 98308

commit v4 on v3

--- a/solution.py
+++ b/solution.py
@@ -247,6 +247,12 @@
         out_ref[:, h * HEAD_DIM:(h + 1) * HEAD_DIM] = turn(h).astype(out_ref.dtype)
     for c in sent:
         c.wait_send()
+
+
+def finish(append_ref, rows_ref, pool_ref, fresh_ref, out_ref, updated_ref):
+    out_ref[...] = rows_ref[...]
+    updated_ref[...] = pool_ref[...]
+    updated_ref[append_ref[0, 0], 0:fresh_ref.shape[0]] = fresh_ref[...]
 
 
 def local(n_inst, n_aa, queries, new_kv, pool, page_table, ctx_len, move_page, move_dest, append_page):
@@ -293,11 +299,20 @@
             dma((far, share - 1, kv_heads)), dma((far, share - 1, kv_heads)),
             dma, dma,
         ],
-        compiler_params=pltpu.CompilerParams(collective_id=0, has_side_effects=True),
+        compiler_params=pltpu.CompilerParams(collective_id=0, has_side_effects=True, vmem_limit_bytes=32 * 2**20),
         name="paged_attention",
     )(page_table, ctx_len, move_page, move_dest, queries[0], pool_pages, fresh_rows)
-    zero = jnp.zeros((), jnp.int32)
-    updated = lax.dynamic_update_slice(pool_pages, fresh_rows[None], (append_page[0, 0], zero, zero, zero))
+    attended, updated = pl.pallas_call(
+        finish,
+        out_shape=(
+            jax.ShapeDtypeStruct(attended.shape, bf),
+            jax.ShapeDtypeStruct(pool_pages.shape, bf),
+        ),
+        in_specs=[pl.BlockSpec(memory_space=pltpu.SMEM)] + [pl.BlockSpec(memory_space=pltpu.VMEM)] * 3,
+        out_specs=(pl.BlockSpec(memory_space=pltpu.VMEM),) * 2,
+        compiler_params=pltpu.CompilerParams(vmem_limit_bytes=12 * 2**20),
+        name="finish",
+    )(append_page, attended, pool_pages, fresh_rows)
     return (attended[None], updated[None])
 
 

time: 33.5 us -> 32.1 us (0.958)
  local copies, waits for them, and re-layouts: 4.52 us -> 3.41 us
  Pallas kernels: 26.8 us -> 26.4 us
    pallas_call x1, Pallas kernels: 26.8 us -> 25.5 us  [local(): pl.pallas_call(functools.partial(kernel, n_inst, n_aa, kv_heads), out_sha...]
    pallas_call x0 -> x1, Pallas kernels: none -> 0.94 us  [local(): pl.pallas_call(finish, out_shape=(jax.ShapeDtypeStruct(attended.shape, bf...]
    dynamic_update_slice x1 -> x0, local copies, waits for them, and re-layouts: 0.64 us -> none  [local(): lax.dynamic_update_slice(pool_pages, fresh_rows[None], (append_page[0, 0]...]
    unnamed x4 -> x12, local copies, waits for them, and re-layouts: 3.87 us -> 3.41 us
where the time goes in v4:
time: 32.1 us; the launch traced here: 31.8 us
  Pallas kernels  26.4 us (82%)
  local copies, waits for them, and re-layouts  3.41 us (11%)
  between operations  1.96 us (6%)
    pallas_call x1, Pallas kernels, local(): pl.pallas_call(functools.partial(kernel, n_inst, n_aa, kv_heads), out_sha...  25.5 us
    unnamed x12, local copies, waits for them, and re-layouts  3.41 us
    pallas_call x1, Pallas kernels, local(): pl.pallas_call(finish, out_shape=(jax.ShapeDtypeStruct(attended.shape, bf...  0.94 us

profile of v4, /device:TPU:0, one launch (start us, length us, event | category | flops | bytes accessed | tf_op | source)
XLA Modules:
  0.0 31.8 jit_solution(1465323169411387150)
XLA Ops:
  1.9 0.0 copy-start.3
  1.9 0.0 copy-start.4
  1.9 0.0 copy-start.5
  2.0 0.6 %copy-done.3 = s32[1,4]{1,0:T(1,128)S(1)} copy-done((s32[1,4]{1,0:T(1,128)S(1)}, s32[1,4]{1,0:T(1,128)}, u32[]{:S(2)}) %copy-start.3) | copy-done | bytes 40
  2.6 0.0 copy-done.4
  2.6 0.0 copy-done.5
  2.6 0.0 copy-start
  2.6 1.0 %copy-done = bf16[1,8,32,2,512]{4,3,2,1,0:T(2,128)(2,1)S(1)} copy-done((bf16[1,8,32,2,512]{4,3,2,1,0:T(2,128)(2,1)S(1)}, bf16[1,8,32,2,512]{4,3,2,1,0:T(2,128)(2,1)}, u32[]{:S(2)}) %copy-start) | copy-done | bytes 524312
  3.7 0.0 copy-start.1
  3.7 0.9 %copy-done.1 = bf16[1,128,1024]{2,1,0:T(8,128)(2,1)S(1)} copy-done((bf16[1,128,1024]{2,1,0:T(8,128)(2,1)S(1)}, bf16[1,128,1024]{2,1,0:T(8,128)(2,1)}, u32[]{:S(2)}) %copy-start.1) | copy-done | bytes 262168
  4.6 0.0 copy-start.2
  4.6 0.8 %copy-done.2 = bf16[1,16,2,512]{3,2,1,0:T(2,128)(2,1)S(1)} copy-done((bf16[1,16,2,512]{3,2,1,0:T(2,128)(2,1)S(1)}, bf16[1,16,2,512]{3,2,1,0:T(2,128)(2,1)}, u32[]{:S(2)}) %copy-start.2) | copy-done | bytes 32792
  5.4 25.5 %paged_attention.1.rows_ref = bf16[128,1024]{1,0:T(8,128)(2,1)S(1)} custom-call(s32[1,4]{1,0:T(1,128)S(1)} %copy-done.3, s32[1,1]{1,0:T(1,128)S(6)} %copy.10.len_ref, s32[1,3]{1,0:T(1,128)S(1)} %copy-done.4, s32[1,3]{1,0:T(1,128)S(1)} %copy-done.5, bf16[128,1024]{1,0:T(8,128)(2,1)S(1)} %bitcast.7, bf16[8,32,2,512]{3,2,1,0:T(2,128)(2,1)S(1)} %bitcast.5, ...), custom_call_target="tpu_custom_call" | custom-call | tf_op jit(solution)/shard_map/paged_attention/pallas_call | solution.py:272
  30.9 0.9 %finish.1 = (bf16[128,1024]{1,0:T(8,128)(2,1)}, bf16[8,32,2,512]{3,2,1,0:T(2,128)(2,1)}) custom-call(s32[1,1]{1,0:T(1,128)S(6)} %copy.11.append_ref, bf16[128,1024]{1,0:T(8,128)(2,1)S(1)} %paged_attention.1.rows_ref, bf16[8,32,2,512]{3,2,1,0:T(2,128)(2,1)S(1)} %bitcast.6, bf16[16,2,512]{2,1,0:T(2,128)(2,1)S(1)} %bitcast.9), custom_call_target="tpu_custom_call" | custom-call | tf_op jit(solution)/shard_map/finish/pallas_call | solution.py:305
Async XLA Ops:
  1.9 0.7 %copy-start.3 = (s32[1,4]{1,0:T(1,128)S(1)}, s32[1,4]{1,0:T(1,128)}, u32[]{:S(2)}) copy-start(s32[1,4]{1,0:T(1,128)} %table_ref.1) | copy-start | bytes 52
  1.9 0.7 %copy-start.4 = (s32[1,3]{1,0:T(1,128)S(1)}, s32[1,3]{1,0:T(1,128)}, u32[]{:S(2)}) copy-start(s32[1,3]{1,0:T(1,128)} %page_ref.1) | copy-start | bytes 40
  1.9 0.7 %copy-start.5 = (s32[1,3]{1,0:T(1,128)S(1)}, s32[1,3]{1,0:T(1,128)}, u32[]{:S(2)}) copy-start(s32[1,3]{1,0:T(1,128)} %dest_ref.1) | copy-start | bytes 40
  2.6 1.0 %copy-start = (bf16[1,8,32,2,512]{4,3,2,1,0:T(2,128)(2,1)S(1)}, bf16[1,8,32,2,512]{4,3,2,1,0:T(2,128)(2,1)}, u32[]{:S(2)}) copy-start(bf16[1,8,32,2,512]{4,3,2,1,0:T(2,128)(2,1)} %param.10) | copy-start | bytes 1572868
  3.7 0.9 %copy-start.1 = (bf16[1,128,1024]{2,1,0:T(8,128)(2,1)S(1)}, bf16[1,128,1024]{2,1,0:T(8,128)(2,1)}, u32[]{:S(2)}) copy-start(bf16[1,128,1024]{2,1,0:T(8,128)(2,1)} %param.8) | copy-start | bytes 786436
  4.6 0.8 %copy-start.2 = (bf16[1,16,2,512]{3,2,1,0:T(2,128)(2,1)S(1)}, bf16[1,16,2,512]{3,2,1,0:T(2,128)(2,1)}, u32[]{:S(2)}) copy-start(bf16[1,16,2,512]{3,2,1,0:T(2,128)(2,1)} %param.9) | copy-start | bytes 98308
